TPU v7x, 32 devices: a whole 2x2x4 slice. The times are simulated.
32 devices in a mesh: req: 2 (over y), blk: 4 (over z), uly: 4 (over x, core).
Axes of the slice: x: 2, y: 2, z: 4, core: 2. Of those that a mesh axis runs over, the one named last changes fastest.
Arguments:
- video_qkv: bfloat16 [3, 2048, 3072], P(None, ('req', 'blk', 'uly')), parts along dimension 1, may hold values from -16 to 16
- text_qkv: bfloat16 [3, 64, 3072], P(None, ('req', 'blk', 'uly')), parts along dimension 1, may hold values from -9.5625 to 9.5625
- video_gate: float32 [6144], P('req'), parts along dimension 0, may hold values from 1 to 4
- text_gate: float32 [6144], P('req'), parts along dimension 0, may hold values from 1 to 4
Outputs:
- video_out: bfloat16 [2048, 3072], P(('req', 'blk', 'uly')), parts along dimension 0
- text_out: bfloat16 [64, 3072], P(('req', 'blk', 'uly')), parts along dimension 0
There are 2 independent parts, one for each index of `req`. A program takes and returns all parts, laid end to end along the dimension named above; each array names one. Nothing has to cross between parts.
All inputs are finite; a program needn't handle non-finite values.
Results may differ from a plain program's by a relative error of at most 0.0085.
Values may be sent and summed in bfloat16 or wider, within the bound.
No kernel may reach another device: no remote copies, remote signals or barrier semaphores. Data moves between devices by JAX's collectives and lax.ppermute only.
A program may use at most 128 MiB of HBM per device.

v0:
```python
import math
import jax
import jax.numpy as jnp
from jax import lax
from jax.sharding import PartitionSpec as P

HEADS = 24
HD = 128


def merge_block(state, queries, block_pair):
    best, total, summed = state
    scale = 1.0 / math.sqrt(queries.shape[-1])
    scores = (
        jnp.einsum("qhd,khd->hqk", queries, block_pair[0], preferred_element_type=jnp.float32)
        * scale
    )
    new_best = jnp.maximum(best, jnp.max(scores, axis=2))
    factor = jnp.exp(best - new_best)
    raised = jnp.exp(scores - new_best[:, :, None])
    total = total * factor + jnp.sum(raised, axis=2)
    product = jnp.einsum(
        "hqk,khd->hqd",
        raised.astype(jnp.bfloat16),
        block_pair[1],
        preferred_element_type=jnp.float32,
    )
    summed = summed * factor[:, :, None] + product
    return (new_best, total, summed)


def attend(video_heads, text_heads):
    heads = video_heads.shape[3]
    width = video_heads.shape[4]
    rows_video = video_heads.shape[1]
    rows_text = text_heads.shape[1]
    joined = jnp.concatenate((video_heads, text_heads), axis=1)
    rows_all = rows_video + rows_text
    joined = joined.reshape(3, rows_all, heads, width)
    queries = joined[0]
    key_pairs = joined[1:]
    initial = (
        jnp.full((heads, rows_all), -jnp.inf, jnp.float32),
        jnp.zeros((heads, rows_all), jnp.float32),
        jnp.zeros((heads, rows_all, width), jnp.float32),
    )
    piece = lax.all_gather(key_pairs, "blk", axis=1, tiled=True)
    count = piece.shape[1] // rows_all

    def one_block(index, inner):
        block_pair = lax.dynamic_slice_in_dim(piece, index * rows_all, rows_all, 1)
        return merge_block(inner, queries, block_pair)

    best, total, summed = lax.fori_loop(0, count, one_block, initial)
    attended = (summed / total[:, :, None]).transpose(1, 0, 2).astype(jnp.bfloat16)
    video_att = attended[:rows_video].reshape(rows_video, 1, heads, width)
    text_att = attended[rows_video:].reshape(rows_text, 1, heads, width)
    return (video_att, text_att)


def on_device(video_qkv, text_qkv, video_gate, text_gate):
    groups = lax.axis_size("uly")
    local_heads = HEADS // groups
    video_rows = video_qkv.shape[1]
    text_rows = text_qkv.shape[1]
    video_split = video_qkv.reshape(3, video_rows, groups, local_heads, HD)
    text_split = text_qkv.reshape(3, text_rows, groups, local_heads, HD)
    video_heads, text_heads = (
        lax.all_to_all(video_split, "uly", split_axis=2, concat_axis=1, tiled=True),
        lax.all_to_all(text_split, "uly", split_axis=2, concat_axis=1, tiled=True),
    )
    video_att, text_att = attend(video_heads, text_heads)
    video_back, text_back = (
        lax.all_to_all(video_att, "uly", split_axis=0, concat_axis=1, tiled=True),
        lax.all_to_all(text_att, "uly", split_axis=0, concat_axis=1, tiled=True),
    )
    video_flat = video_back.reshape(video_rows, HEADS * HD).astype(jnp.float32)
    text_flat = text_back.reshape(text_rows, HEADS * HD).astype(jnp.float32)
    video_out = (video_flat * video_gate[None, :]).astype(jnp.bfloat16)
    text_out = (text_flat * text_gate[None, :]).astype(jnp.bfloat16)
    return (video_out, text_out)


def solution(mesh):
    in_specs = (
        P(None, ("req", "blk", "uly"), None),
        P(None, ("req", "blk", "uly"), None),
        P("req"),
        P("req"),
    )
    out_specs = (P(("req", "blk", "uly"), None), P(("req", "blk", "uly"), None))
    return jax.shard_map(
        on_device, mesh=mesh, in_specs=in_specs, out_specs=out_specs, check_vma=False
    )
```

profile of v0, /device:TPU:0, one launch (start us, length us, event | category | flops | bytes accessed | tf_op | source)
XLA Modules:
  0.0 148.8 jit_solution(10764639887761051975)
XLA Ops:
  7.2 0.8 reshape.38
  8.0 0.6 copy.22
  8.6 4.2 %all-to-all-start.1 = ((bf16[3,2,4,6,128]{4,1,3,0,2:T(2,128)(2,1)}), bf16[3,2,4,6,128]{4,1,3,0,2:T(2,128)(2,1)S(1)}, u32[]{:S(2)}, u32[]{:S(2)}) async-start(bf16[3,2,4,6,128]{4,1,3,0,2:T(2,128)(2,1)} %copy.22), calls=%async_computation.1 | async-start | bytes 73728 | tf_op jit(solution)/shard_map/all_to_all | solution.py:70
  12.9 2.8 %reshape.37 = bf16[3,64,4,6,128]{4,3,2,1,0:T(8,128)(2,1)S(1)} reshape(bf16[3,64,3072]{2,1,0:T(8,128)(2,1)} %param.6) | data formatting | bytes 2359296 | tf_op jit(solution)/shard_map/reshape | solution.py:66
  15.7 1.5 copy.20
  17.2 0.0 all-to-all-done.1
  17.2 3.5 %all-to-all-start = ((bf16[3,64,4,6,128]{4,1,3,0,2:T(8,128)(2,1)}), bf16[3,64,4,6,128]{4,1,3,0,2:T(8,128)(2,1)S(1)}, u32[]{:S(2)}, u32[]{:S(2)}) async-start(bf16[3,64,4,6,128]{4,1,3,0,2:T(8,128)(2,1)} %copy.20), calls=%async_computation | async-start | bytes 2359296 | tf_op jit(solution)/shard_map/all_to_all | solution.py:69
  20.7 0.0 all-gather.3.cloned.1.call-start
  20.8 15.7 %all-to-all-done = bf16[3,64,4,6,128]{4,1,3,0,2:T(8,128)(2,1)S(1)} async-done(((bf16[3,64,4,6,128]{4,1,3,0,2:T(8,128)(2,1)}), bf16[3,64,4,6,128]{4,1,3,0,2:T(8,128)(2,1)S(1)}, u32[]{:S(2)}, u32[]{:S(2)}) %all-to-all-start) | async-done | bytes 1179680 | tf_op jit(solution)/shard_map/all_to_all | solution.py:69
  36.5 0.1 copy.21
  36.6 1.0 fusion.12
  37.6 0.0 all-gather.3.cloned.1.call-update
  37.7 66.0 %all-gather.3.cloned.1.call-done = bf16[2,1056,1,6,128]{4,1,3,0,2:T(8,128)(2,1)} async-done(((bf16[2,264,1,6,128]{4,1,3,0,2:T(8,128)(2,1)}), bf16[2,1056,1,6,128]{4,1,3,0,2:T(8,128)(2,1)}) %all-gather.3.cloned.1.call-update) | async-done | bytes 3244048 | tf_op jit(solution)/shard_map/all_gather | solution.py:47
  103.7 16.6 %while.18 = (s32[]{:T(128)}, f32[6,264]{1,0:T(8,128)S(1)}, f32[6,264]{1,0:T(8,128)S(1)}, f32[6,264,128]{2,1,0:T(8,128)S(1)}, bf16[2,1056,6,128]{3,1,2,0:T(8,128)...) while((s32[]{:T(128)}, f32[6,264]{1,0:T(8,128)S(1)}, ...), condition=%wide.region_3.0_spmd.clone, body=%wide.region_0.0_spmd.clone.sunk | while | flops 218067712 | bytes 7958215 | solution.py:54
  103.7 1.6 %bitcast_reduce_fusion.2 = (f32[6,264]{1,0:T(8,128)S(1)}, f32[6,264,264]{2,1,0:T(8,128)S(1)}) fusion(bf16[264,6,128]{2,0,1:T(8,128)(2,1)S(1)} %get-tuple-element.223, bf16[2,1056,6,128]{3,1,2,0:T(8,128)(2,1)} %get-tuple-element.222, s32[]{:T(128)S(6)} %select_n.9), kind=kOutput, calls=%fused_computation.1.clone.1 | convolution fusion | flops 107887824 | bytes 2490052 | tf_op jit(solution)/shard_map/while/body/eval_jaxpr/qhd,khd->hqk/dot_general | solution.py:15
  105.3 0.4 fusion.24
  105.8 2.0 %convolution_add_fusion.2 = f32[6,264,128]{2,1,0:T(8,128)S(1)} fusion(f32[6,264,264]{2,1,0:T(8,128)S(1)} %get-tuple-element.193, f32[6,264]{1,0:T(8,128)S(1)} %select_maximum_fusion.2, f32[6,264,128]{2,1,0:T(8,128)S(1)} %get-tuple-element.210, bf16[2,1056,6,128]{3,1,2,0:T(8,128)(2,1)} %get-tuple-element.222, s32[]{:T(128)S(6)} %add.53, ...), kind=kOutput, calls=%fused_computation.5.clone.1 | convolution fusion | flops 108915840 | bytes 3712905 | tf_op jit(solution)/shard_map/while/body/eval_jaxpr/hqk,khd->hqd/dot_general | solution.py:22
  107.8 1.6 %bitcast_reduce_fusion.2 = (f32[6,264]{1,0:T(8,128)S(1)}, f32[6,264,264]{2,1,0:T(8,128)S(1)}) fusion(bf16[264,6,128]{2,0,1:T(8,128)(2,1)S(1)} %get-tuple-element.223, bf16[2,1056,6,128]{3,1,2,0:T(8,128)(2,1)} %get-tuple-element.222, s32[]{:T(128)S(6)} %select_n.9), kind=kOutput, calls=%fused_computation.1.clone.1 | convolution fusion | flops 107887824 | bytes 2490052 | tf_op jit(solution)/shard_map/while/body/eval_jaxpr/qhd,khd->hqk/dot_general | solution.py:15
  109.5 0.4 fusion.24
  109.9 2.0 %convolution_add_fusion.2 = f32[6,264,128]{2,1,0:T(8,128)S(1)} fusion(f32[6,264,264]{2,1,0:T(8,128)S(1)} %get-tuple-element.193, f32[6,264]{1,0:T(8,128)S(1)} %select_maximum_fusion.2, f32[6,264,128]{2,1,0:T(8,128)S(1)} %get-tuple-element.210, bf16[2,1056,6,128]{3,1,2,0:T(8,128)(2,1)} %get-tuple-element.222, s32[]{:T(128)S(6)} %add.53, ...), kind=kOutput, calls=%fused_computation.5.clone.1 | convolution fusion | flops 108915840 | bytes 3712905 | tf_op jit(solution)/shard_map/while/body/eval_jaxpr/hqk,khd->hqd/dot_general | solution.py:22
  112.0 1.6 %bitcast_reduce_fusion.2 = (f32[6,264]{1,0:T(8,128)S(1)}, f32[6,264,264]{2,1,0:T(8,128)S(1)}) fusion(bf16[264,6,128]{2,0,1:T(8,128)(2,1)S(1)} %get-tuple-element.223, bf16[2,1056,6,128]{3,1,2,0:T(8,128)(2,1)} %get-tuple-element.222, s32[]{:T(128)S(6)} %select_n.9), kind=kOutput, calls=%fused_computation.1.clone.1 | convolution fusion | flops 107887824 | bytes 2490052 | tf_op jit(solution)/shard_map/while/body/eval_jaxpr/qhd,khd->hqk/dot_general | solution.py:15
  113.6 0.4 fusion.24
  114.1 2.0 %convolution_add_fusion.2 = f32[6,264,128]{2,1,0:T(8,128)S(1)} fusion(f32[6,264,264]{2,1,0:T(8,128)S(1)} %get-tuple-element.193, f32[6,264]{1,0:T(8,128)S(1)} %select_maximum_fusion.2, f32[6,264,128]{2,1,0:T(8,128)S(1)} %get-tuple-element.210, bf16[2,1056,6,128]{3,1,2,0:T(8,128)(2,1)} %get-tuple-element.222, s32[]{:T(128)S(6)} %add.53, ...), kind=kOutput, calls=%fused_computation.5.clone.1 | convolution fusion | flops 108915840 | bytes 3712905 | tf_op jit(solution)/shard_map/while/body/eval_jaxpr/hqk,khd->hqd/dot_general | solution.py:22
  116.2 1.6 %bitcast_reduce_fusion.2 = (f32[6,264]{1,0:T(8,128)S(1)}, f32[6,264,264]{2,1,0:T(8,128)S(1)}) fusion(bf16[264,6,128]{2,0,1:T(8,128)(2,1)S(1)} %get-tuple-element.223, bf16[2,1056,6,128]{3,1,2,0:T(8,128)(2,1)} %get-tuple-element.222, s32[]{:T(128)S(6)} %select_n.9), kind=kOutput, calls=%fused_computation.1.clone.1 | convolution fusion | flops 107887824 | bytes 2490052 | tf_op jit(solution)/shard_map/while/body/eval_jaxpr/qhd,khd->hqk/dot_general | solution.py:15
  117.8 0.4 fusion.24
  118.3 2.0 %convolution_add_fusion.2 = f32[6,264,128]{2,1,0:T(8,128)S(1)} fusion(f32[6,264,264]{2,1,0:T(8,128)S(1)} %get-tuple-element.193, f32[6,264]{1,0:T(8,128)S(1)} %select_maximum_fusion.2, f32[6,264,128]{2,1,0:T(8,128)S(1)} %get-tuple-element.210, bf16[2,1056,6,128]{3,1,2,0:T(8,128)(2,1)} %get-tuple-element.222, s32[]{:T(128)S(6)} %add.53, ...), kind=kOutput, calls=%fused_computation.5.clone.1 | convolution fusion | flops 108915840 | bytes 3712905 | tf_op jit(solution)/shard_map/while/body/eval_jaxpr/hqk,khd->hqd/dot_general | solution.py:22
  120.3 0.0 copy-start.1
  120.3 0.1 copy.24
  120.5 0.4 fusion.13
  120.8 0.6 slice_bitcast_fusion.1
  121.4 3.3 %all-to-all-start.3 = ((bf16[8,1,6,128]{3,2,1,0:T(8,128)(2,1)}), bf16[8,1,6,128]{3,2,1,0:T(8,128)(2,1)S(1)}, u32[]{:S(2)}, u32[]{:S(2)}) async-start(bf16[8,1,6,128]{3,2,1,0:T(8,128)(2,1)} %slice_bitcast_fusion.1), calls=%async_computation.3 | async-start | bytes 32768 | tf_op jit(solution)/shard_map/all_to_all | solution.py:75
  124.7 0.8 slice_bitcast_fusion
  125.5 0.0 copy-start
  125.5 3.0 %all-to-all-done.3 = bf16[8,1,6,128]{3,2,1,0:T(8,128)(2,1)S(1)} async-done(((bf16[8,1,6,128]{3,2,1,0:T(8,128)(2,1)}), bf16[8,1,6,128]{3,2,1,0:T(8,128)(2,1)S(1)}, u32[]{:S(2)}, u32[]{:S(2)}) %all-to-all-start.3) | async-done | bytes 12320 | tf_op jit(solution)/shard_map/all_to_all | solution.py:75
  128.5 3.5 %all-to-all-start.2 = ((bf16[256,1,6,128]{3,2,1,0:T(8,128)(2,1)}), bf16[256,1,6,128]{3,2,1,0:T(8,128)(2,1)S(1)}, u32[]{:S(2)}, u32[]{:S(2)}) async-start(bf16[256,1,6,128]{3,2,1,0:T(8,128)(2,1)} %slice_bitcast_fusion), calls=%async_computation.2 | async-start | bytes 1048576 | tf_op jit(solution)/shard_map/all_to_all | solution.py:74
  132.0 0.0 copy-done.1
  132.0 0.6 multiply_convert_fusion.1
  132.7 8.1 %all-to-all-done.2 = bf16[256,1,6,128]{3,2,1,0:T(8,128)(2,1)S(1)} async-done(((bf16[256,1,6,128]{3,2,1,0:T(8,128)(2,1)}), bf16[256,1,6,128]{3,2,1,0:T(8,128)(2,1)S(1)}, u32[]{:S(2)}, u32[]{:S(2)}) %all-to-all-start.2) | async-done | bytes 393248 | tf_op jit(solution)/shard_map/all_to_all | solution.py:74
  140.8 0.1 copy_bitcast_fusion
  140.9 0.2 reshape.41
  141.1 0.0 copy-done
  141.1 0.8 multiply_convert_fusion
  (19 shorter events, 0.2 us)
Async XLA Ops:
  8.6 8.6 %all-to-all-start.1 = ((bf16[3,2,4,6,128]{4,1,3,0,2:T(2,128)(2,1)}), bf16[3,2,4,6,128]{4,1,3,0,2:T(2,128)(2,1)S(1)}, u32[]{:S(2)}, u32[]{:S(2)}) async-start(bf16[3,2,4,6,128]{4,1,3,0,2:T(2,128)(2,1)} %copy.22), calls=%async_computation.1 | async-start | bytes 73728 | tf_op jit(solution)/shard_map/all_to_all | solution.py:70
  17.2 19.3 %all-to-all-start = ((bf16[3,64,4,6,128]{4,1,3,0,2:T(8,128)(2,1)}), bf16[3,64,4,6,128]{4,1,3,0,2:T(8,128)(2,1)S(1)}, u32[]{:S(2)}, u32[]{:S(2)}) async-start(bf16[3,64,4,6,128]{4,1,3,0,2:T(8,128)(2,1)} %copy.20), calls=%async_computation | async-start | bytes 2359296 | tf_op jit(solution)/shard_map/all_to_all | solution.py:69
  20.7 83.0 %all-gather.3.cloned.1.call-start = ((), (), s32[]{:S(2)}) async-start(), calls=%async_computation.4 | async-start | bytes 4055040 | tf_op jit(solution)/shard_map/all_gather | solution.py:47
  120.3 11.7 %copy-start.1 = (f32[3072]{0:T(1024)S(1)}, f32[3072]{0:T(1024)}, u32[]{:S(2)}) copy-start(f32[3072]{0:T(1024)} %param.9) | copy-start | bytes 36868
  121.4 7.1 %all-to-all-start.3 = ((bf16[8,1,6,128]{3,2,1,0:T(8,128)(2,1)}), bf16[8,1,6,128]{3,2,1,0:T(8,128)(2,1)S(1)}, u32[]{:S(2)}, u32[]{:S(2)}) async-start(bf16[8,1,6,128]{3,2,1,0:T(8,128)(2,1)} %slice_bitcast_fusion.1), calls=%async_computation.3 | async-start | bytes 32768 | tf_op jit(solution)/shard_map/all_to_all | solution.py:75
  125.5 15.6 %copy-start = (f32[3072]{0:T(1024)S(1)}, f32[3072]{0:T(1024)}, u32[]{:S(2)}) copy-start(f32[3072]{0:T(1024)} %param.8) | copy-start | bytes 36868
  128.5 12.3 %all-to-all-start.2 = ((bf16[256,1,6,128]{3,2,1,0:T(8,128)(2,1)}), bf16[256,1,6,128]{3,2,1,0:T(8,128)(2,1)S(1)}, u32[]{:S(2)}, u32[]{:S(2)}) async-start(bf16[256,1,6,128]{3,2,1,0:T(8,128)(2,1)} %slice_bitcast_fusion), calls=%async_computation.2 | async-start | bytes 1048576 | tf_op jit(solution)/shard_map/all_to_all | solution.py:74
Sparse Core Ops, SparseCore 0:
  37.7 65.8 all-gather.2
where the time goes:
time: 150 us; the launch traced here: 149 us
  waiting for transfers between devices  92.8 us (62%)
  starting transfers between devices  14.5 us (10%)
  matrix products  14.5 us (10%)
  between operations  14.2 us (9%)
  local copies, waits for them, and re-layouts  7.71 us (5%)
  other arithmetic  4.76 us (3%)
    all_gather x1, waiting for transfers between devices, attend(): piece = lax.all_gather(key_pairs, 'blk', axis=1, tiled=True)  66 us
    all_to_all x1, waiting for transfers between devices, on_device(): lax.all_to_all(video_split, 'uly', split_axis=2, concat_axis=1, tiled=True)  15.7 us
    all_to_all x1, waiting for transfers between devices, on_device(): lax.all_to_all(video_att, 'uly', split_axis=0, concat_axis=1, tiled=True)  8.12 us
    dot_general x4, matrix products, merge_block(): jnp.einsum('hqk,khd->hqd', raised.astype(jnp.bfloat16), block_pair[1], pr...  8.08 us
    dot_general x4, matrix products, merge_block(): jnp.einsum('qhd,khd->hqk', queries, block_pair[0], preferred_element_type...  6.46 us
    reshape x2, local copies, waits for them, and re-layouts, on_device(): video_split = video_qkv.reshape(3, video_rows, groups, local_heads, HD)  4.32 us
    all_to_all x1, starting transfers between devices, on_device(): lax.all_to_all(text_split, 'uly', split_axis=2, concat_axis=1, tiled=True)  4.24 us
    all_to_all x1, starting transfers between devices, on_device(): lax.all_to_all(video_split, 'uly', split_axis=2, concat_axis=1, tiled=True)  3.53 us
  transfers between devices with their start and end apart: 5, of which 4 were waited for; matrix products, arithmetic and copies ran while one was open for 4% of the time, Pallas kernels for 0%

commit v1 on v0

--- a/solution.py
+++ b/solution.py
@@ -71,7 +71,12 @@
     )
     video_att, text_att = attend(video_heads, text_heads)
     video_back, text_back = (
-        lax.all_to_all(video_att, "uly", split_axis=0, concat_axis=1, tiled=True),
+        jnp.concatenate(
+            lax.all_to_all(
+                jnp.stack(jnp.split(video_att, lax.axis_size("uly"), axis=0)), "uly", 0, 0
+            ),
+            axis=1,
+        ),
         lax.all_to_all(text_att, "uly", split_axis=0, concat_axis=1, tiled=True),
     )
     video_flat = video_back.reshape(video_rows, HEADS * HD).astype(jnp.float32)

time: 150 us -> 148 us (0.987)
  no operation moved by 1% of the time
where the time goes in v1:
time: 148 us
  waiting for transfers between devices  91.5 us (62%)
  starting transfers between devices  14.5 us (10%)
  matrix products  14.5 us (10%)
  between operations  14.2 us (10%)
  local copies, waits for them, and re-layouts  7.25 us (5%)
  other arithmetic  5.45 us (4%)
    all_gather x1, waiting for transfers between devices, attend(): piece = lax.all_gather(key_pairs, 'blk', axis=1, tiled=True)  66 us
    all_to_all x1, waiting for transfers between devices, on_device(): lax.all_to_all(video_split, 'uly', split_axis=2, concat_axis=1, tiled=True)  15.7 us
    dot_general x4, matrix products, merge_block(): jnp.einsum('hqk,khd->hqd', raised.astype(jnp.bfloat16), block_pair[1], pr...  8.08 us
    all_to_all x1, waiting for transfers between devices, on_device(): lax.all_to_all(jnp.stack(jnp.split(video_att, lax.axis_size('uly'), axis=...  6.71 us
    dot_general x4, matrix products, merge_block(): jnp.einsum('qhd,khd->hqk', queries, block_pair[0], preferred_element_type...  6.46 us
    reshape x2, local copies, waits for them, and re-layouts, on_device(): video_split = video_qkv.reshape(3, video_rows, groups, local_heads, HD)  4.32 us
    all_to_all x1, starting transfers between devices, on_device(): lax.all_to_all(text_split, 'uly', split_axis=2, concat_axis=1, tiled=True)  4.24 us
    all_to_all x1, starting transfers between devices, on_device(): lax.all_to_all(video_split, 'uly', split_axis=2, concat_axis=1, tiled=True)  3.53 us
  transfers between devices with their start and end apart: 5, of which 4 were waited for; matrix products, arithmetic and copies ran while one was open for 4% of the time, Pallas kernels for 0%

profile of v1, /device:TPU:0, one launch (start us, length us, event | category | flops | bytes accessed | tf_op | source)
XLA Modules:
  0.0 147.6 jit_solution(3872706208251128937)
XLA Ops:
  7.2 0.8 reshape.41
  8.0 0.6 copy.31
  8.6 4.2 %all-to-all-start.1 = ((bf16[3,2,4,6,128]{4,1,3,0,2:T(2,128)(2,1)}), bf16[3,2,4,6,128]{4,1,3,0,2:T(2,128)(2,1)S(1)}, u32[]{:S(2)}, u32[]{:S(2)}) async-start(bf16[3,2,4,6,128]{4,1,3,0,2:T(2,128)(2,1)} %copy.31), calls=%async_computation.1 | async-start | bytes 73728 | tf_op jit(solution)/shard_map/all_to_all | solution.py:70
  12.9 2.8 %reshape.40 = bf16[3,64,4,6,128]{4,3,2,1,0:T(8,128)(2,1)S(1)} reshape(bf16[3,64,3072]{2,1,0:T(8,128)(2,1)} %param.6) | data formatting | bytes 2359296 | tf_op jit(solution)/shard_map/reshape | solution.py:66
  15.7 1.5 %copy.29 = bf16[3,64,4,6,128]{4,1,3,0,2:T(8,128)(2,1)} copy(bf16[3,64,4,6,128]{4,3,2,1,0:T(8,128)(2,1)S(1)} %reshape.40) | data formatting | bytes 2359296 | tf_op jit(solution)/shard_map/reshape | solution.py:66
  17.2 0.0 all-to-all-done.1
  17.2 3.5 %all-to-all-start = ((bf16[3,64,4,6,128]{4,1,3,0,2:T(8,128)(2,1)}), bf16[3,64,4,6,128]{4,1,3,0,2:T(8,128)(2,1)S(1)}, u32[]{:S(2)}, u32[]{:S(2)}) async-start(bf16[3,64,4,6,128]{4,1,3,0,2:T(8,128)(2,1)} %copy.29), calls=%async_computation | async-start | bytes 2359296 | tf_op jit(solution)/shard_map/all_to_all | solution.py:69
  20.7 0.0 all-gather.3.cloned.1.call-start
  20.8 15.7 %all-to-all-done = bf16[3,64,4,6,128]{4,1,3,0,2:T(8,128)(2,1)S(1)} async-done(((bf16[3,64,4,6,128]{4,1,3,0,2:T(8,128)(2,1)}), bf16[3,64,4,6,128]{4,1,3,0,2:T(8,128)(2,1)S(1)}, u32[]{:S(2)}, u32[]{:S(2)}) %all-to-all-start) | async-done | bytes 1179680 | tf_op jit(solution)/shard_map/all_to_all | solution.py:69
  36.5 0.1 copy.30
  36.6 1.0 fusion.11
  37.6 0.0 all-gather.3.cloned.1.call-update
  37.7 66.0 %all-gather.3.cloned.1.call-done = bf16[2,1056,1,6,128]{4,1,3,0,2:T(8,128)(2,1)} async-done(((bf16[2,264,1,6,128]{4,1,3,0,2:T(8,128)(2,1)}), bf16[2,1056,1,6,128]{4,1,3,0,2:T(8,128)(2,1)}) %all-gather.3.cloned.1.call-update) | async-done | bytes 3244048 | tf_op jit(solution)/shard_map/all_gather | solution.py:47
  103.7 16.6 %while.18 = (s32[]{:T(128)}, f32[6,264]{1,0:T(8,128)S(1)}, f32[6,264]{1,0:T(8,128)S(1)}, f32[6,264,128]{2,1,0:T(8,128)S(1)}, bf16[2,1056,6,128]{3,1,2,0:T(8,128)...) while((s32[]{:T(128)}, f32[6,264]{1,0:T(8,128)S(1)}, ...), condition=%wide.region_3.0_spmd.clone, body=%wide.region_0.0_spmd.clone.sunk | while | flops 218067712 | bytes 7958215 | solution.py:54
  103.7 1.6 %bitcast_reduce_fusion.2 = (f32[6,264]{1,0:T(8,128)S(1)}, f32[6,264,264]{2,1,0:T(8,128)S(1)}) fusion(bf16[264,6,128]{2,0,1:T(8,128)(2,1)S(1)} %get-tuple-element.227, bf16[2,1056,6,128]{3,1,2,0:T(8,128)(2,1)} %get-tuple-element.226, s32[]{:T(128)S(6)} %select_n.9), kind=kOutput, calls=%fused_computation.1.clone.1 | convolution fusion | flops 107887824 | bytes 2490052 | tf_op jit(solution)/shard_map/while/body/eval_jaxpr/qhd,khd->hqk/dot_general | solution.py:15
  105.3 0.4 fusion.22
  105.8 2.0 %convolution_add_fusion.2 = f32[6,264,128]{2,1,0:T(8,128)S(1)} fusion(f32[6,264,264]{2,1,0:T(8,128)S(1)} %get-tuple-element.197, f32[6,264]{1,0:T(8,128)S(1)} %select_maximum_fusion.2, f32[6,264,128]{2,1,0:T(8,128)S(1)} %get-tuple-element.214, bf16[2,1056,6,128]{3,1,2,0:T(8,128)(2,1)} %get-tuple-element.226, s32[]{:T(128)S(6)} %add.53, ...), kind=kOutput, calls=%fused_computation.5.clone.1 | convolution fusion | flops 108915840 | bytes 3712905 | tf_op jit(solution)/shard_map/while/body/eval_jaxpr/hqk,khd->hqd/dot_general | solution.py:22
  107.9 1.6 %bitcast_reduce_fusion.2 = (f32[6,264]{1,0:T(8,128)S(1)}, f32[6,264,264]{2,1,0:T(8,128)S(1)}) fusion(bf16[264,6,128]{2,0,1:T(8,128)(2,1)S(1)} %get-tuple-element.227, bf16[2,1056,6,128]{3,1,2,0:T(8,128)(2,1)} %get-tuple-element.226, s32[]{:T(128)S(6)} %select_n.9), kind=kOutput, calls=%fused_computation.1.clone.1 | convolution fusion | flops 107887824 | bytes 2490052 | tf_op jit(solution)/shard_map/while/body/eval_jaxpr/qhd,khd->hqk/dot_general | solution.py:15
  109.5 0.4 fusion.22
  110.0 2.0 %convolution_add_fusion.2 = f32[6,264,128]{2,1,0:T(8,128)S(1)} fusion(f32[6,264,264]{2,1,0:T(8,128)S(1)} %get-tuple-element.197, f32[6,264]{1,0:T(8,128)S(1)} %select_maximum_fusion.2, f32[6,264,128]{2,1,0:T(8,128)S(1)} %get-tuple-element.214, bf16[2,1056,6,128]{3,1,2,0:T(8,128)(2,1)} %get-tuple-element.226, s32[]{:T(128)S(6)} %add.53, ...), kind=kOutput, calls=%fused_computation.5.clone.1 | convolution fusion | flops 108915840 | bytes 3712905 | tf_op jit(solution)/shard_map/while/body/eval_jaxpr/hqk,khd->hqd/dot_general | solution.py:22
  112.0 1.6 %bitcast_reduce_fusion.2 = (f32[6,264]{1,0:T(8,128)S(1)}, f32[6,264,264]{2,1,0:T(8,128)S(1)}) fusion(bf16[264,6,128]{2,0,1:T(8,128)(2,1)S(1)} %get-tuple-element.227, bf16[2,1056,6,128]{3,1,2,0:T(8,128)(2,1)} %get-tuple-element.226, s32[]{:T(128)S(6)} %select_n.9), kind=kOutput, calls=%fused_computation.1.clone.1 | convolution fusion | flops 107887824 | bytes 2490052 | tf_op jit(solution)/shard_map/while/body/eval_jaxpr/qhd,khd->hqk/dot_general | solution.py:15
  113.6 0.4 fusion.22
  114.1 2.0 %convolution_add_fusion.2 = f32[6,264,128]{2,1,0:T(8,128)S(1)} fusion(f32[6,264,264]{2,1,0:T(8,128)S(1)} %get-tuple-element.197, f32[6,264]{1,0:T(8,128)S(1)} %select_maximum_fusion.2, f32[6,264,128]{2,1,0:T(8,128)S(1)} %get-tuple-element.214, bf16[2,1056,6,128]{3,1,2,0:T(8,128)(2,1)} %get-tuple-element.226, s32[]{:T(128)S(6)} %add.53, ...), kind=kOutput, calls=%fused_computation.5.clone.1 | convolution fusion | flops 108915840 | bytes 3712905 | tf_op jit(solution)/shard_map/while/body/eval_jaxpr/hqk,khd->hqd/dot_general | solution.py:22
  116.2 1.6 %bitcast_reduce_fusion.2 = (f32[6,264]{1,0:T(8,128)S(1)}, f32[6,264,264]{2,1,0:T(8,128)S(1)}) fusion(bf16[264,6,128]{2,0,1:T(8,128)(2,1)S(1)} %get-tuple-element.227, bf16[2,1056,6,128]{3,1,2,0:T(8,128)(2,1)} %get-tuple-element.226, s32[]{:T(128)S(6)} %select_n.9), kind=kOutput, calls=%fused_computation.1.clone.1 | convolution fusion | flops 107887824 | bytes 2490052 | tf_op jit(solution)/shard_map/while/body/eval_jaxpr/qhd,khd->hqk/dot_general | solution.py:15
  117.8 0.4 fusion.22
  118.3 2.0 %convolution_add_fusion.2 = f32[6,264,128]{2,1,0:T(8,128)S(1)} fusion(f32[6,264,264]{2,1,0:T(8,128)S(1)} %get-tuple-element.197, f32[6,264]{1,0:T(8,128)S(1)} %select_maximum_fusion.2, f32[6,264,128]{2,1,0:T(8,128)S(1)} %get-tuple-element.214, bf16[2,1056,6,128]{3,1,2,0:T(8,128)(2,1)} %get-tuple-element.226, s32[]{:T(128)S(6)} %add.53, ...), kind=kOutput, calls=%fused_computation.5.clone.1 | convolution fusion | flops 108915840 | bytes 3712905 | tf_op jit(solution)/shard_map/while/body/eval_jaxpr/hqk,khd->hqd/dot_general | solution.py:22
  120.3 0.0 copy-start.1
  120.3 0.3 fusion.13
  120.7 0.6 copy.34
  121.3 3.2 %all-to-all-start.3 = ((bf16[8,1,6,128]{3,2,1,0:T(8,128)(2,1)}), bf16[8,1,6,128]{3,2,1,0:T(8,128)(2,1)S(1)}, u32[]{:S(2)}, u32[]{:S(2)}) async-start(bf16[8,1,6,128]{3,2,1,0:T(8,128)(2,1)} %copy.34), calls=%async_computation.3 | async-start | bytes 32768 | tf_op jit(solution)/shard_map/all_to_all | solution.py:80
  124.5 0.8 pad_maximum_fusion.1
  125.3 3.0 %all-to-all-done.3 = bf16[8,1,6,128]{3,2,1,0:T(8,128)(2,1)S(1)} async-done(((bf16[8,1,6,128]{3,2,1,0:T(8,128)(2,1)}), bf16[8,1,6,128]{3,2,1,0:T(8,128)(2,1)S(1)}, u32[]{:S(2)}, u32[]{:S(2)}) %all-to-all-start.3) | async-done | bytes 12320 | tf_op jit(solution)/shard_map/all_to_all | solution.py:80
  128.3 3.5 %all-to-all-start.2 = ((bf16[4,64,1,6,128]{4,1,3,2,0:T(8,128)(2,1)}), bf16[4,64,1,6,128]{4,1,3,2,0:T(8,128)(2,1)S(1)}, u32[]{:S(2)}, u32[]{:S(2)}) async-start(bf16[4,64,1,6,128]{4,1,3,2,0:T(8,128)(2,1)} %pad_maximum_fusion.1), calls=%async_computation.2 | async-start | bytes 786432 | tf_op jit(solution)/shard_map/all_to_all | solution.py:75
  131.9 0.0 copy-done.1
  131.9 0.6 multiply_convert_fusion.1
  132.5 0.0 copy-start
  132.5 6.7 %all-to-all-done.2 = bf16[4,64,1,6,128]{4,1,3,2,0:T(8,128)(2,1)S(1)} async-done(((bf16[4,64,1,6,128]{4,1,3,2,0:T(8,128)(2,1)}), bf16[4,64,1,6,128]{4,1,3,2,0:T(8,128)(2,1)S(1)}, u32[]{:S(2)}, u32[]{:S(2)}) %all-to-all-start.2) | async-done | bytes 393248 | tf_op jit(solution)/shard_map/all_to_all | solution.py:75
  139.2 0.1 convert_bitcast_fusion
  139.3 0.5 copy.33
  139.8 0.2 reshape.43
  139.9 0.0 copy-done
  140.0 0.8 multiply_convert_fusion
  (21 shorter events, 0.2 us)
Async XLA Ops:
  8.6 8.6 %all-to-all-start.1 = ((bf16[3,2,4,6,128]{4,1,3,0,2:T(2,128)(2,1)}), bf16[3,2,4,6,128]{4,1,3,0,2:T(2,128)(2,1)S(1)}, u32[]{:S(2)}, u32[]{:S(2)}) async-start(bf16[3,2,4,6,128]{4,1,3,0,2:T(2,128)(2,1)} %copy.31), calls=%async_computation.1 | async-start | bytes 73728 | tf_op jit(solution)/shard_map/all_to_all | solution.py:70
  17.2 19.3 %all-to-all-start = ((bf16[3,64,4,6,128]{4,1,3,0,2:T(8,128)(2,1)}), bf16[3,64,4,6,128]{4,1,3,0,2:T(8,128)(2,1)S(1)}, u32[]{:S(2)}, u32[]{:S(2)}) async-start(bf16[3,64,4,6,128]{4,1,3,0,2:T(8,128)(2,1)} %copy.29), calls=%async_computation | async-start | bytes 2359296 | tf_op jit(solution)/shard_map/all_to_all | solution.py:69
  20.7 83.0 %all-gather.3.cloned.1.call-start = ((), (), s32[]{:S(2)}) async-start(), calls=%async_computation.4 | async-start | bytes 4055040 | tf_op jit(solution)/shard_map/all_gather | solution.py:47
  120.3 11.5 %copy-start.1 = (f32[3072]{0:T(1024)S(1)}, f32[3072]{0:T(1024)}, u32[]{:S(2)}) copy-start(f32[3072]{0:T(1024)} %param.9) | copy-start | bytes 36868
  121.3 7.1 %all-to-all-start.3 = ((bf16[8,1,6,128]{3,2,1,0:T(8,128)(2,1)}), bf16[8,1,6,128]{3,2,1,0:T(8,128)(2,1)S(1)}, u32[]{:S(2)}, u32[]{:S(2)}) async-start(bf16[8,1,6,128]{3,2,1,0:T(8,128)(2,1)} %copy.34), calls=%async_computation.3 | async-start | bytes 32768 | tf_op jit(solution)/shard_map/all_to_all | solution.py:80
  128.3 10.8 %all-to-all-start.2 = ((bf16[4,64,1,6,128]{4,1,3,2,0:T(8,128)(2,1)}), bf16[4,64,1,6,128]{4,1,3,2,0:T(8,128)(2,1)S(1)}, u32[]{:S(2)}, u32[]{:S(2)}) async-start(bf16[4,64,1,6,128]{4,1,3,2,0:T(8,128)(2,1)} %pad_maximum_fusion.1), calls=%async_computation.2 | async-start | bytes 786432 | tf_op jit(solution)/shard_map/all_to_all | solution.py:75
  132.5 7.5 %copy-start = (f32[3072]{0:T(1024)S(1)}, f32[3072]{0:T(1024)}, u32[]{:S(2)}) copy-start(f32[3072]{0:T(1024)} %param.8) | copy-start | bytes 36868
Sparse Core Ops, SparseCore 0:
  37.8 65.8 all-gather.2
